TPU v7x, 128 devices: a whole 4x4x4 slice. The times are simulated.
128 devices in a mesh: gx: 4 (over y), gy: 4 (over z_hi, core), gz: 8 (over z_lo, x).
Axes of the slice: x: 4, y: 4, z: 4 (z_hi: 2, z_lo: 2; z = z_hi * 2 + z_lo), core: 2. Of those that a mesh axis runs over, the one named last changes fastest.
Arguments:
- volume: bfloat16 [32, 32, 32, 32, 128], P('gx', 'gy', 'gz'), may hold values from -6 to 6
- conv_kernel: bfloat16 [3, 3, 3, 32, 64], replicated, may hold values from -0.21875 to 0.21875
- dense_one: bfloat16 [16, 16, 16, 64, 2048], P('gx', None, None, ('gy', 'gz')), may hold values from -0.01171875 to 0.01171875
- dense_two: float32 [2048, 256], replicated, may hold values from -0.125 to 0.125
- dense_three: float32 [256, 4], replicated, may hold values from -0.375 to 0.375
- targets: float32 [4, 128], replicated, may hold values from -3 to 3
Outputs:
- prediction: float32 [4, 128], replicated
- grad_dense_one: bfloat16 [16, 16, 16, 64, 2048], P('gx', None, None, ('gy', 'gz'))
- grad_conv: float32 [3, 3, 3, 32, 64], replicated
- grad_volume: bfloat16 [32, 32, 32, 32, 128], P('gx', 'gy', 'gz')
All inputs are finite; a program needn't handle non-finite values.
Results may differ from a plain program's by a relative error of at most 0.008.
Values may be sent and summed in bfloat16 or wider, within the bound.
A program may use at most 128 MiB of HBM per device.

v0:
```python
import jax
import jax.numpy as jnp
from jax import lax
from jax.sharding import PartitionSpec as P

loss_scale = 1024.0
leak_slope = 0.3


def with_halo(array, sides, width):
    for axis, dim in sides:
        size, length = (lax.axis_size(axis), array.shape[dim])
        up = [(i, (i + 1) % size) for i in range(size - 1)]
        down = [(j, i) for i, j in up]
        last = lax.slice_in_dim(array, length - width, length, axis=dim)
        initial = lax.slice_in_dim(array, 0, width, axis=dim)
        before = lax.ppermute(last, axis, up)
        after = lax.ppermute(initial, axis, down)
        array = jnp.concatenate([before, array, after], axis=dim)
    return array


def from_behind(block, axis, distance):
    devices = range(lax.axis_size(axis))
    route = [(i - distance, i) for i in devices if i - distance in devices]
    return lax.ppermute(block, axis, route)


def shortened(array):
    return jax.tree.map(lambda a: a.astype(jnp.bfloat16) if a.dtype == jnp.float32 else a, array)


def smooth_leaky(values):
    return leak_slope * values + (1.0 - leak_slope) * jax.nn.softplus(values)


def leaky_derivative(values):
    return leak_slope + (1.0 - leak_slope) * jax.nn.sigmoid(values)


def conv_forward(padded, kernel):
    return lax.conv_general_dilated(
        padded,
        kernel,
        (1, 1, 1),
        "VALID",
        dimension_numbers=("DHWCN", "DHWIO", "DHWCN"),
        preferred_element_type=jnp.float32,
    )


def conv_back_input(padded_grad, kernel):
    flipped = kernel[::-1, ::-1, ::-1]
    return lax.conv_general_dilated(
        padded_grad,
        flipped,
        (1, 1, 1),
        "VALID",
        dimension_numbers=("DHWCN", "DHWOI", "DHWCN"),
        preferred_element_type=jnp.float32,
    )


def conv_back_kernel(padded, gradient):
    return lax.conv_general_dilated(
        padded,
        gradient,
        (1, 1, 1),
        "VALID",
        dimension_numbers=("DHWNC", "DHWOI", "DHWNC"),
        preferred_element_type=jnp.float32,
    )


def pooling(values):
    extent_x, extent_y, extent_z, channels, samples = values.shape
    return values.reshape(
        extent_x // 2, 2, extent_y // 2, 2, extent_z // 2, 2, channels, samples
    ).mean(axis=(1, 3, 5))


def spread(values):
    extent_x, extent_y, extent_z, channels, samples = values.shape
    widened = jnp.broadcast_to(
        values[:, None, :, None, :, None],
        (extent_x, 2, extent_y, 2, extent_z, 2, channels, samples),
    )
    return widened.reshape(2 * extent_x, 2 * extent_y, 2 * extent_z, channels, samples)


def fold_faces(inner, from_below, from_above, axis_dim):
    length = inner.shape[axis_dim]
    first = lax.slice_in_dim(inner, 0, 1, axis=axis_dim) + from_below
    middle = lax.slice_in_dim(inner, 1, length - 1, axis=axis_dim)
    last = lax.slice_in_dim(inner, length - 1, length, axis=axis_dim) + from_above
    return jnp.concatenate([first, middle, last], axis=axis_dim)


def body(volume, conv_kernel, dense_one, dense_two, dense_three, targets):
    padded = with_halo(volume, (("gx", 0), ("gy", 1), ("gz", 2)), 1)
    conv_out = conv_forward(padded, conv_kernel)
    pooled = pooling(smooth_leaky(conv_out)).astype(jnp.bfloat16)
    half_x, half_y, half_z, channels, samples = pooled.shape
    groups_y = lax.axis_size("gy")
    groups_z = lax.axis_size("gz")
    per_group = channels // (groups_y * groups_z)
    arrived = lax.all_to_all(pooled[None], ("gy", "gz"), split_axis=4, concat_axis=0, tiled=True)
    arrived = arrived.reshape(groups_y, groups_z, half_x, half_y, half_z, per_group, samples)
    weights_local = dense_one.reshape(
        half_x, groups_y, half_y, groups_z, half_z, per_group, dense_one.shape[4]
    )
    partial_one = jnp.einsum(
        "uvxyzcb,xuyvzch->hb", arrived, weights_local, preferred_element_type=jnp.float32
    )
    pre_one = lax.psum(partial_one, ("gx", "gy", "gz"))
    hidden_one = smooth_leaky(pre_one)
    pre_two = jnp.dot(dense_two.T, hidden_one, precision=lax.Precision.HIGHEST)
    hidden_two = smooth_leaky(pre_two)
    prediction = jnp.dot(dense_three.T, hidden_two, precision=lax.Precision.HIGHEST)
    error_grad = loss_scale * (prediction - targets)
    grad_pre_two = jnp.dot(
        dense_three, error_grad, precision=lax.Precision.HIGHEST
    ) * leaky_derivative(pre_two)
    grad_pre_one = (
        jnp.dot(dense_two, grad_pre_two, precision=lax.Precision.HIGHEST)
        * leaky_derivative(pre_one)
    ).astype(jnp.bfloat16)
    grad_local = jnp.einsum(
        "uvxyzcb,hb->xuyvzch", arrived, grad_pre_one, preferred_element_type=jnp.float32
    )
    grad_dense_one = (grad_local / samples).astype(jnp.bfloat16).reshape(dense_one.shape)
    grad_arrived = jnp.einsum(
        "xuyvzch,hb->uvxyzcb", weights_local, grad_pre_one, preferred_element_type=jnp.float32
    ).astype(jnp.bfloat16)
    outgoing = grad_arrived.reshape(groups_y * groups_z, half_x, half_y, half_z, per_group, samples)
    returned = lax.all_to_all(outgoing, ("gy", "gz"), split_axis=0, concat_axis=4, tiled=True)
    grad_pooled = returned.reshape(half_x, half_y, half_z, channels, samples)
    grad_out = (spread(grad_pooled.astype(jnp.float32)) / 8.0 * leaky_derivative(conv_out)).astype(
        jnp.bfloat16
    )
    widened = jnp.pad(grad_out, ((2, 2), (2, 2), (2, 2), (0, 0), (0, 0)))
    whole = conv_back_input(widened, conv_kernel)
    below_x = from_behind(whole[-1:].astype(jnp.bfloat16), "gx", 1).astype(jnp.float32)
    above_x = from_behind(whole[:1].astype(jnp.bfloat16), "gx", -1).astype(jnp.float32)
    folded = fold_faces(whole[1:-1], below_x, above_x, 0)
    below_y = from_behind(shortened(folded[:, -1:]), "gy", 1)
    above_y = from_behind(shortened(folded[:, :1]), "gy", -1)
    folded = fold_faces(folded[:, 1:-1], below_y, above_y, 1)
    below_z = from_behind(shortened(folded[:, :, -1:]), "gz", 1)
    above_z = from_behind(shortened(folded[:, :, :1]), "gz", -1)
    folded = fold_faces(folded[:, :, 1:-1], below_z, above_z, 2)
    grad_volume = folded.astype(jnp.bfloat16)
    kernel_local = conv_back_kernel(padded, grad_out)
    grad_conv = lax.psum(kernel_local, ("gx", "gy", "gz")) / samples
    return (prediction, grad_dense_one, grad_conv, grad_volume)


def solution(mesh):
    return jax.shard_map(
        body,
        mesh=mesh,
        in_specs=(
            P("gx", "gy", "gz", None, None),
            P(),
            P("gx", None, None, ("gy", "gz"), None),
            P(),
            P(),
            P(),
        ),
        out_specs=(
            P(),
            P("gx", None, None, ("gy", "gz"), None),
            P(),
            P("gx", "gy", "gz", None, None),
        ),
        check_vma=False,
    )
```

profile of v0, /device:TPU:1, one launch (start us, length us, event | category | flops | bytes accessed | tf_op | source)
XLA Modules:
  0.0 538.4 jit_solution(12310446413016146924)
XLA Ops:
  8.4 4.0 collective-permute-start
  13.8 3.7 collective-permute-done
  21.4 7.2 %collective-permute-start.2 = (bf16[10,1,4,32,128]{4,3,2,1,0:T(8,128)(2,1)S(1)}, bf16[10,1,4,32,128]{4,3,2,1,0:T(8,128)(2,1)S(1)}, u32[]{:S(2)}, u32[]{:S(2)}) collective-permute-start(bf16[10,1,4,32,128]{4,3,2,1,0:T(8,128)(2,1)S(1)} %get-tuple-element.18), channel_id=1, source_target_pairs={{0,8},{8,16},{16,24},{1,9},{9,17},{17,25},{2,10},{10,18},{18,26},{... | collective-permute-start | bytes 983048 | tf_op jit(solution)/shard_map/ppermute | solution.py:17
  32.6 23.5 %collective-permute-done.3 = bf16[10,1,4,32,128]{4,3,2,1,0:T(8,128)(2,1)S(1)} collective-permute-done((bf16[10,1,4,32,128]{4,3,2,1,0:T(8,128)(2,1)S(1)}, bf16[10,1,4,32,128]{4,3,2,1,0:T(8,128)(2,1)S(1)}, u32[]{:S(2)}, u32[]{:S(2)}) %collective-permute-start.3) | collective-permute-done | bytes 327712 | tf_op jit(solution)/shard_map/ppermute | solution.py:18
  58.9 7.9 %collective-permute-done.4 = bf16[10,10,1,32,128]{4,3,2,1,0:T(8,128)(2,1)S(1)} collective-permute-done((bf16[10,10,1,32,128]{4,3,2,1,0:T(8,128)(2,1)S(1)}, bf16[10,10,1,32,128]{4,3,2,1,0:T(8,128)(2,1)S(1)}, u32[]{:S(2)}, u32[]{:S(2)}) %collective-permute-start.4) | collective-permute-done | bytes 819232 | tf_op jit(solution)/shard_map/ppermute | solution.py:17
  66.8 3.9 collective-permute-done.5
  70.7 18.1 %fusion.2 = (f32[8,8,4,64,128]{4,3,2,1,0:T(8,128)}, f32[8,8,4,64,128]{4,3,2,1,0:T(8,128)}) fusion(bf16[3,3,3,32,64]{4,3,2,1,0:T(8,128)(2,1)S(1)} %copy-done.12, bf16[10,10,1,32,128]{4,3,2,1,0:T(8,128)(2,1)S(1)} %collective-permute-done.5, bf16[10,1,4,32,128]{4,3,2,1,0:T(8,128)(2,1)S(1)} %collective-permute-done.3, ...), kind=kOutput, calls=%fused_computation.4 | convolution fusion | flops 3652583424 | bytes 21803008 | tf_op jit(solution)/shard_map/conv_general_dilated | solution.py:42
  88.8 4.4 reduce_sum.9
  93.9 13.4 %all_to_all.24 = bf16[1,4,4,2,64,128]{5,3,2,1,0,4:T(2,128)(2,1)S(1)} all-to-all(bf16[1,4,4,2,64,128]{5,3,2,1,0,4:T(2,128)(2,1)S(1)} %copy.45), channel_id=1, replica_groups=mesh['gx'=4,'gy'=4,'gz'=8] {'gy','gz'}, dimensions={4} | all-to-all | bytes 1048576 | tf_op jit(solution)/shard_map/all_to_all | solution.py:107
  107.6 13.7 %fusion.7 = f32[2048,128]{0,1:T(8,128)} fusion(bf16[4,4,4,8,2,2,2048]{6,5,4,3,2,1,0:T(2,128)(2,1)} %bitcast.72, bf16[32,1,4,4,2,2,128]{6,5,0,4,3,2,1:T(2,128)(2,1)S(1)} %bitcast.70), kind=kOutput, calls=%fused_computation.14 | convolution fusion | flops 1073741824 | bytes 9961472 | tf_op jit(solution)/shard_map/uvxyzcb,xuyvzch->hb/dot_general | solution.py:112
  121.6 145.5 %all-reduce.3.cloned.1.call-done = f32[2048,128]{0,1:T(8,128)} async-done(((f32[2048,128]{0,1:T(8,128)}), f32[2048,128]{0,1:T(8,128)}) %all-reduce.3.cloned.1.call-update) | async-done | bytes 1048592 | tf_op jit(solution)/shard_map/psum | solution.py:115
  270.7 3.5 fusion.12
  274.3 8.6 %fusion.16 = bf16[4,8,4,4,2,2,128]{6,1,5,4,3,0,2:T(8,128)(2,1)S(1)} fusion(bf16[2048,128,1,1,1,1,1]{0,1,6,5,4,3,2:T(8,128)(2,1)S(1)} %fusion.12, bf16[4,4,4,8,2,2,2048]{6,5,4,3,2,1,0:T(2,128)(2,1)} %bitcast.73), kind=kOutput, calls=%fused_computation.21 | convolution fusion | flops 1074003968 | bytes 9437184 | tf_op jit(solution)/shard_map/xuyvzch,hb->uvxyzcb/dot_general | solution.py:132
  283.6 17.6 %all_to_all.25 = bf16[32,4,4,2,2,128]{5,4,3,2,1,0:T(2,128)(2,1)S(1)} all-to-all(bf16[32,4,4,2,2,128]{5,4,3,2,1,0:T(2,128)(2,1)S(1)} %copy.56), channel_id=1, replica_groups=mesh['gx'=4,'gy'=4,'gz'=8] {'gy','gz'}, dimensions={0} | all-to-all | bytes 1048576 | tf_op jit(solution)/shard_map/all_to_all | solution.py:136
  307.3 29.9 %fusion.70 = (bf16[10,10,6,32,128]{4,3,2,1,0:T(8,128)(2,1)S(1)}, f32[10,10,6,32,128]{4,3,2,1,0:T(8,128)S(1)}) fusion(bf16[8,8,4,64,128]{4,3,2,1,0:T(8,128)(2,1)S(1)} %multiply_convert_fusion.1, bf16[3,3,3,32,64]{4,3,2,1,0:T(8,128)(2,1)S(1)} %copy-done.13), kind=kOutput, calls=%fused_computation.92 | convolution fusion | flops 3626336256 | bytes 19050496 | tf_op jit(solution)/shard_map/conv_general_dilated | solution.py:54
  341.8 7.6 %collective-permute-done.6 = bf16[1,10,6,32,128]{4,3,2,1,0:T(8,128)(2,1)S(1)} collective-permute-done((bf16[1,10,6,32,128]{4,3,2,1,0:T(8,128)(2,1)S(1)}, bf16[1,10,6,32,128]{4,3,2,1,0:T(8,128)(2,1)S(1)}, u32[]{:S(2)}, u32[]{:S(2)}) %collective-permute-start.6) | collective-permute-done | bytes 491552 | tf_op jit(solution)/shard_map/ppermute | solution.py:26
  349.4 3.9 collective-permute-done.7
  354.4 4.0 collective-permute-start.8
  360.6 15.5 %fusion.61 = f32[3,3,3,32,64]{4,3,2,1,0:T(8,128)} fusion(bf16[8,8,4,64,128]{4,3,2,1,0:T(8,128)(2,1)S(1)} %multiply_convert_fusion.1, bf16[10,10,1,32,128]{4,3,2,1,0:T(8,128)(2,1)S(1)} %copy-done.17, bf16[10,1,4,32,128]{4,3,2,1,0:T(8,128)(2,1)S(1)} %copy-done.11, bf16[10,8,4,32,128]{4,3,2,1,0:T(8,128)(2,1)S(1)} %copy-done.7, ...), kind=kOutput, calls=%fused_computation.83 | convolution fusion | flops 3633709056 | bytes 9330688 | tf_op jit(solution)/shard_map/conv_general_dilated | solution.py:65
  376.1 3.5 pad_maximum_fusion
  383.9 3.0 collective-permute-start.10
  390.7 9.4 %copy.52 = bf16[4,4,4,8,2,2,2048]{6,5,4,3,2,1,0:T(2,128)(2,1)} copy(bf16[4,4,4,8,2,2,2048]{6,3,5,4,2,0,1:T(8,128)(2,1)S(1)} %fusion) | data formatting | bytes 16777216 | tf_op jit(solution)/shard_map/convert_element_type | solution.py:131
  400.0 122.7 %all-reduce.5.cloned.1.call-done = f32[3,3,3,32,64]{4,3,2,1,0:T(8,128)} async-done(((f32[3,3,3,32,64]{4,3,2,1,0:T(8,128)}), f32[3,3,3,32,64]{4,3,2,1,0:T(8,128)}) %all-reduce.5.cloned.1.call-update) | async-done | bytes 221200 | tf_op jit(solution)/shard_map/psum | solution.py:154
  524.6 3.4 pad_maximum_fusion.1
  (102 shorter events, 45.7 us)
Async XLA Ops:
  7.2 259.9 %copy-start = (f32[2048,256]{1,0:T(8,128)S(1)}, f32[2048,256]{1,0:T(8,128)}, u32[]{:S(2)}) copy-start(f32[2048,256]{1,0:T(8,128)} %param.9) | copy-start | bytes 6291460
  7.2 259.9 %all-reduce.3.cloned.1.call-start = ((), (), s32[]{:S(2)}) async-start(), calls=%async_computation.2 | async-start | bytes 2097152 | tf_op jit(solution)/shard_map/psum | solution.py:115
  8.4 9.0 %collective-permute-start = (bf16[1,8,4,32,128]{4,3,2,1,0:T(8,128)(2,1)S(1)}, bf16[1,8,4,32,128]{4,3,2,1,0:T(8,128)(2,1)S(1)}, u32[]{:S(2)}, u32[]{:S(2)}) collective-permute-start(bf16[1,8,4,32,128]{4,3,2,1,0:T(8,128)(2,1)S(1)} %get-tuple-element.21), channel_id=1, source_target_pairs={{0,32},{32,64},{64,96},{1,33},{33,65},{65,97},{2,34},{34,66},{66,9... | collective-permute-start | bytes 786440 | tf_op jit(solution)/shard_map/ppermute | solution.py:17
  12.5 8.8 %collective-permute-start.1 = (bf16[1,8,4,32,128]{4,3,2,1,0:T(8,128)(2,1)S(1)}, bf16[1,8,4,32,128]{4,3,2,1,0:T(8,128)(2,1)S(1)}, u32[]{:S(2)}, u32[]{:S(2)}) collective-permute-start(bf16[1,8,4,32,128]{4,3,2,1,0:T(8,128)(2,1)S(1)} %get-tuple-element.20), channel_id=1, source_target_pairs={{32,0},{64,32},{96,64},{33,1},{65,33},{97,65},{34,2},{66,34},{98,6... | collective-permute-start | bytes 786440 | tf_op jit(solution)/shard_map/ppermute | solution.py:18
  17.5 53.2 %copy-start.12 = (bf16[3,3,3,32,64]{4,3,2,1,0:T(8,128)(2,1)S(1)}, bf16[3,3,3,32,64]{4,3,2,1,0:T(8,128)(2,1)}, u32[]{:S(2)}) copy-start(bf16[3,3,3,32,64]{4,3,2,1,0:T(8,128)(2,1)} %param.7) | copy-start | bytes 331780
  21.3 67.4 %copy-start.6 = (bf16[10,8,4,32,128]{4,3,2,1,0:T(8,128)(2,1)}, bf16[10,8,4,32,128]{4,3,2,1,0:T(8,128)(2,1)S(1)}, u32[]{:S(2)}) copy-start(bf16[10,8,4,32,128]{4,3,2,1,0:T(8,128)(2,1)S(1)} %constant_dynamic-update-slice_fusion) | copy-start | bytes 7864324
  21.4 11.2 %collective-permute-start.2 = (bf16[10,1,4,32,128]{4,3,2,1,0:T(8,128)(2,1)S(1)}, bf16[10,1,4,32,128]{4,3,2,1,0:T(8,128)(2,1)S(1)}, u32[]{:S(2)}, u32[]{:S(2)}) collective-permute-start(bf16[10,1,4,32,128]{4,3,2,1,0:T(8,128)(2,1)S(1)} %get-tuple-element.18), channel_id=1, source_target_pairs={{0,8},{8,16},{16,24},{1,9},{9,17},{17,25},{2,10},{10,18},{18,26},{... | collective-permute-start | bytes 983048 | tf_op jit(solution)/shard_map/ppermute | solution.py:17
  28.6 27.5 %collective-permute-start.3 = (bf16[10,1,4,32,128]{4,3,2,1,0:T(8,128)(2,1)S(1)}, bf16[10,1,4,32,128]{4,3,2,1,0:T(8,128)(2,1)S(1)}, u32[]{:S(2)}, u32[]{:S(2)}) collective-permute-start(bf16[10,1,4,32,128]{4,3,2,1,0:T(8,128)(2,1)S(1)} %get-tuple-element.19), channel_id=1, source_target_pairs={{8,0},{16,8},{24,16},{9,1},{17,9},{25,17},{10,2},{18,10},{26,18},{... | collective-permute-start | bytes 983048 | tf_op jit(solution)/shard_map/ppermute | solution.py:18
  32.6 56.2 %copy-start.8 = (bf16[10,1,4,32,128]{4,3,2,1,0:T(8,128)(2,1)}, bf16[10,1,4,32,128]{4,3,2,1,0:T(8,128)(2,1)S(1)}, u32[]{:S(2)}) copy-start(bf16[10,1,4,32,128]{4,3,2,1,0:T(8,128)(2,1)S(1)} %collective-permute-done.2) | copy-start | bytes 983044
  56.1 32.7 %copy-start.10 = (bf16[10,1,4,32,128]{4,3,2,1,0:T(8,128)(2,1)}, bf16[10,1,4,32,128]{4,3,2,1,0:T(8,128)(2,1)S(1)}, u32[]{:S(2)}) copy-start(bf16[10,1,4,32,128]{4,3,2,1,0:T(8,128)(2,1)S(1)} %collective-permute-done.3) | copy-start | bytes 983044
  56.3 10.6 %collective-permute-start.4 = (bf16[10,10,1,32,128]{4,3,2,1,0:T(8,128)(2,1)S(1)}, bf16[10,10,1,32,128]{4,3,2,1,0:T(8,128)(2,1)S(1)}, u32[]{:S(2)}, u32[]{:S(2)}) collective-permute-start(bf16[10,10,1,32,128]{4,3,2,1,0:T(8,128)(2,1)S(1)} %get-tuple-element.14), channel_id=1, source_target_pairs={{0,1},{1,2},{2,3},{3,4},{4,5},{5,6},{6,7},{8,9},{9,10},{10,11},{11... | collective-permute-start | bytes 2457608 | tf_op jit(solution)/shard_map/ppermute | solution.py:17
  57.6 13.1 %collective-permute-start.5 = (bf16[10,10,1,32,128]{4,3,2,1,0:T(8,128)(2,1)S(1)}, bf16[10,10,1,32,128]{4,3,2,1,0:T(8,128)(2,1)S(1)}, u32[]{:S(2)}, u32[]{:S(2)}) collective-permute-start(bf16[10,10,1,32,128]{4,3,2,1,0:T(8,128)(2,1)S(1)} %get-tuple-element.15), channel_id=1, source_target_pairs={{1,0},{2,1},{3,2},{4,3},{5,4},{6,5},{7,6},{9,8},{10,9},{11,10},{12... | collective-permute-start | bytes 2457608 | tf_op jit(solution)/shard_map/ppermute | solution.py:18
  66.8 22.0 %copy-start.14 = (bf16[10,10,1,32,128]{4,3,2,1,0:T(8,128)(2,1)}, bf16[10,10,1,32,128]{4,3,2,1,0:T(8,128)(2,1)S(1)}, u32[]{:S(2)}) copy-start(bf16[10,10,1,32,128]{4,3,2,1,0:T(8,128)(2,1)S(1)} %collective-permute-done.4) | copy-start | bytes 2457604
  70.7 18.1 %copy-start.16 = (bf16[10,10,1,32,128]{4,3,2,1,0:T(8,128)(2,1)}, bf16[10,10,1,32,128]{4,3,2,1,0:T(8,128)(2,1)S(1)}, u32[]{:S(2)}) copy-start(bf16[10,10,1,32,128]{4,3,2,1,0:T(8,128)(2,1)S(1)} %collective-permute-done.5) | copy-start | bytes 2457604
  107.5 162.5 %copy-start.18 = (f32[256,4]{0,1:T(4,128)S(1)}, f32[256,4]{0,1:T(4,128)}, u32[]{:S(2)}) copy-start(f32[256,4]{0,1:T(4,128)} %param.10) | copy-start | bytes 12292
  107.6 162.8 %copy-start.19 = (f32[4,128]{1,0:T(4,128)S(1)}, f32[4,128]{1,0:T(4,128)}, u32[]{:S(2)}) copy-start(f32[4,128]{1,0:T(4,128)} %param.11) | copy-start | bytes 6148
  121.3 401.4 %all-reduce.5.cloned.1.call-start = ((), (), s32[]{:S(2)}) async-start(), calls=%async_computation.3 | async-start | bytes 884736 | tf_op jit(solution)/shard_map/psum | solution.py:154
  283.0 20.3 %slice-start.1 = ((s8[8388608]{0:T(1024)(128)(4,1)}), s8[4194304]{0:T(1024)(128)(4,1)S(1)}, s32[]{:S(2)}) async-start(s8[8388608]{0:T(1024)(128)(4,1)} %bitcast.65), calls=%async_computation.5 | async-start | bytes 8388608
  337.3 12.2 %collective-permute-start.6 = (bf16[1,10,6,32,128]{4,3,2,1,0:T(8,128)(2,1)S(1)}, bf16[1,10,6,32,128]{4,3,2,1,0:T(8,128)(2,1)S(1)}, u32[]{:S(2)}, u32[]{:S(2)}) collective-permute-start(bf16[1,10,6,32,128]{4,3,2,1,0:T(8,128)(2,1)S(1)} %get-tuple-element.10), channel_id=1, source_target_pairs={{0,32},{32,64},{64,96},{1,33},{33,65},{65,97},{2,34},{34,66},{66,9... | collective-permute-start | bytes 1474568 | tf_op jit(solution)/shard_map/ppermute | solution.py:26
  339.3 14.0 %collective-permute-start.7 = (bf16[1,10,6,32,128]{4,3,2,1,0:T(8,128)(2,1)S(1)}, bf16[1,10,6,32,128]{4,3,2,1,0:T(8,128)(2,1)S(1)}, u32[]{:S(2)}, u32[]{:S(2)}) collective-permute-start(bf16[1,10,6,32,128]{4,3,2,1,0:T(8,128)(2,1)S(1)} %get-tuple-element.11), channel_id=1, source_target_pairs={{32,0},{64,32},{96,64},{33,1},{65,33},{97,65},{34,2},{66,34},{98,6... | collective-permute-start | bytes 1474568 | tf_op jit(solution)/shard_map/ppermute | solution.py:26
  354.4 25.7 %collective-permute-start.8 = (bf16[8,1,6,32,128]{4,3,2,1,0:T(8,128)(2,1)S(1)}, bf16[8,1,6,32,128]{4,3,2,1,0:T(8,128)(2,1)}, u32[]{:S(2)}, u32[]{:S(2)}) collective-permute-start(bf16[8,1,6,32,128]{4,3,2,1,0:T(8,128)(2,1)S(1)} %get-tuple-element.12), channel_id=1, source_target_pairs={{0,8},{8,16},{16,24},{1,9},{9,17},{17,25},{2,10},{10,18},{18,26},{... | collective-permute-start | bytes 1179656 | tf_op jit(solution)/shard_map/ppermute | solution.py:26
  358.4 21.7 %collective-permute-start.9 = (bf16[8,1,6,32,128]{4,3,2,1,0:T(8,128)(2,1)S(1)}, bf16[8,1,6,32,128]{4,3,2,1,0:T(8,128)(2,1)}, u32[]{:S(2)}, u32[]{:S(2)}) collective-permute-start(bf16[8,1,6,32,128]{4,3,2,1,0:T(8,128)(2,1)S(1)} %get-tuple-element.13), channel_id=1, source_target_pairs={{8,0},{16,8},{24,16},{9,1},{17,9},{25,17},{10,2},{18,10},{26,18},{... | collective-permute-start | bytes 1179656 | tf_op jit(solution)/shard_map/ppermute | solution.py:26
  383.9 144.2 %collective-permute-start.10 = (bf16[8,8,1,32,128]{4,3,2,1,0:T(8,128)(2,1)}, bf16[8,8,1,32,128]{4,3,2,1,0:T(8,128)(2,1)}, u32[]{:S(2)}, u32[]{:S(2)}) collective-permute-start(bf16[8,8,1,32,128]{4,3,2,1,0:T(8,128)(2,1)} %get-tuple-element.16), channel_id=1, source_target_pairs={{0,1},{1,2},{2,3},{3,4},{4,5},{5,6},{6,7},{8,9},{9,10},{10,11},{11... | collective-permute-start | bytes 1572872 | tf_op jit(solution)/shard_map/ppermute | solution.py:26
  386.8 141.2 %collective-permute-start.11 = (bf16[8,8,1,32,128]{4,3,2,1,0:T(8,128)(2,1)}, bf16[8,8,1,32,128]{4,3,2,1,0:T(8,128)(2,1)}, u32[]{:S(2)}, u32[]{:S(2)}) collective-permute-start(bf16[8,8,1,32,128]{4,3,2,1,0:T(8,128)(2,1)} %get-tuple-element.17), channel_id=1, source_target_pairs={{1,0},{2,1},{3,2},{4,3},{5,4},{6,5},{7,6},{9,8},{10,9},{11,10},{12... | collective-permute-start | bytes 1572872 | tf_op jit(solution)/shard_map/ppermute | solution.py:26
  (16 other events, 100.1 us)
Sparse Core Ops, SparseCore 0:
  121.4 145.5 all-reduce.2
  376.2 146.5 all-reduce.4
where the time goes:
time: 547 us; the launch traced here: 538 us
  waiting for transfers between devices  322 us (59%)
  matrix products  95.2 us (17%)
  starting transfers between devices  31.3 us (6%)
  blocking collectives  31 us (6%)
  other arithmetic  23.4 us (4%)
  local copies, waits for them, and re-layouts  20.5 us (4%)
  between operations  14.9 us (3%)
    psum x1, waiting for transfers between devices, body(): pre_one = lax.psum(partial_one, ('gx', 'gy', 'gz'))  145 us
    psum x1, waiting for transfers between devices, body(): grad_conv = lax.psum(kernel_local, ('gx', 'gy', 'gz')) / samples  123 us
    conv_general_dilated x1, matrix products, conv_back_input(): lax.conv_general_dilated(padded_grad, flipped, (1, 1, 1), 'VALID', dimens...  29.9 us
    ppermute x3, waiting for transfers between devices, with_halo(): after = lax.ppermute(initial, axis, down)  28.7 us
    conv_general_dilated x1, matrix products, conv_forward(): lax.conv_general_dilated(padded, kernel, (1, 1, 1), 'VALID', dimension_nu...  18.1 us
    all_to_all x1, blocking collectives, body(): lax.all_to_all(outgoing, ('gy', 'gz'), split_axis=0, concat_axis=4, tiled...  17.6 us
    conv_general_dilated x1, matrix products, conv_back_kernel(): lax.conv_general_dilated(padded, gradient, (1, 1, 1), 'VALID', dimension_...  15.5 us
    ppermute x6, starting transfers between devices, from_behind(): return lax.ppermute(block, axis, route)  13.9 us
  transfers between devices with their start and end apart: 14, of which 10 were waited for; matrix products, arithmetic and copies ran while one was open for 8% of the time, Pallas kernels for 0%

commit v1 on v0

--- a/solution.py
+++ b/solution.py
@@ -151,7 +151,7 @@
     folded = fold_faces(folded[:, :, 1:-1], below_z, above_z, 2)
     grad_volume = folded.astype(jnp.bfloat16)
     kernel_local = conv_back_kernel(padded, grad_out)
-    grad_conv = lax.psum(kernel_local, ("gx", "gy", "gz")) / samples
+    grad_conv = jnp.sum(lax.all_gather(kernel_local, ("gx", "gy", "gz")), axis=0) / samples
     return (prediction, grad_dense_one, grad_conv, grad_volume)
 
 

time: 547 us -> 748 us (1.37)
  waiting for transfers between devices: 322 us -> 508 us
  other arithmetic: 23.4 us -> 33.1 us
    all_gather x0 -> x1, waiting for transfers between devices: none -> 292 us  [body(): lax.all_gather(kernel_local, ('gx', 'gy', 'gz'))]
    psum x1 -> x0, waiting for transfers between devices: 123 us -> none  [body(): grad_conv = lax.psum(kernel_local, ('gx', 'gy', 'gz')) / samples]
    reduce_sum x0 -> x1, other arithmetic: none -> 18.2 us  [body(): jnp.sum(lax.all_gather(kernel_local, ('gx', 'gy', 'gz')), axis=0) / samples]
    ppermute x6, waiting for transfers between devices: 11.5 us -> 28 us  [from_behind(): return lax.ppermute(block, axis, route)]
  transfers between devices with their start and end apart: 14 -> 14, of which waited for: 10 -> 12; matrix products, arithmetic and copies ran while one was open for 8% -> 7% of each run, Pallas kernels for 0% -> 0%
where the time goes in v1:
time: 748 us; the launch traced here: 736 us
  waiting for transfers between devices  508 us (68%)
  matrix products  97 us (13%)
  other arithmetic  33.1 us (4%)
  blocking collectives  31.2 us (4%)
  starting transfers between devices  29.1 us (4%)
  local copies, waits for them, and re-layouts  22.5 us (3%)
  between operations  15 us (2%)
    all_gather x1, waiting for transfers between devices, body(): lax.all_gather(kernel_local, ('gx', 'gy', 'gz'))  292 us
    psum x1, waiting for transfers between devices, body(): pre_one = lax.psum(partial_one, ('gx', 'gy', 'gz'))  145 us
    conv_general_dilated x1, matrix products, conv_back_input(): lax.conv_general_dilated(padded_grad, flipped, (1, 1, 1), 'VALID', dimens...  31.7 us
    ppermute x3, waiting for transfers between devices, with_halo(): after = lax.ppermute(initial, axis, down)  28.7 us
    ppermute x6, waiting for transfers between devices, from_behind(): return lax.ppermute(block, axis, route)  28 us
    reduce_sum x1, other arithmetic, body(): jnp.sum(lax.all_gather(kernel_local, ('gx', 'gy', 'gz')), axis=0) / samples  18.2 us
    conv_general_dilated x1, matrix products, conv_forward(): lax.conv_general_dilated(padded, kernel, (1, 1, 1), 'VALID', dimension_nu...  18.1 us
    all_to_all x1, blocking collectives, body(): lax.all_to_all(outgoing, ('gy', 'gz'), split_axis=0, concat_axis=4, tiled...  17.7 us
  transfers between devices with their start and end apart: 14, of which 12 were waited for; matrix products, arithmetic and copies ran while one was open for 7% of the time, Pallas kernels for 0%

profile of v1, /device:TPU:1, one launch (start us, length us, event | category | flops | bytes accessed | tf_op | source)
XLA Modules:
  0.0 735.6 jit_solution(15731468662811332756)
XLA Ops:
  8.4 4.0 collective-permute-start
  13.8 3.7 collective-permute-done
  21.4 7.2 collective-permute-start.2
  32.6 23.5 %collective-permute-done.3 = bf16[10,1,4,32,128]{4,3,2,1,0:T(8,128)(2,1)S(1)} collective-permute-done((bf16[10,1,4,32,128]{4,3,2,1,0:T(8,128)(2,1)S(1)}, bf16[10,1,4,32,128]{4,3,2,1,0:T(8,128)(2,1)S(1)}, u32[]{:S(2)}, u32[]{:S(2)}) %collective-permute-start.3) | collective-permute-done | bytes 327712 | tf_op jit(solution)/shard_map/ppermute | solution.py:18
  58.9 7.9 %collective-permute-done.4 = bf16[10,10,1,32,128]{4,3,2,1,0:T(8,128)(2,1)S(1)} collective-permute-done((bf16[10,10,1,32,128]{4,3,2,1,0:T(8,128)(2,1)S(1)}, bf16[10,10,1,32,128]{4,3,2,1,0:T(8,128)(2,1)S(1)}, u32[]{:S(2)}, u32[]{:S(2)}) %collective-permute-start.4) | collective-permute-done | bytes 819232 | tf_op jit(solution)/shard_map/ppermute | solution.py:17
  66.8 3.9 collective-permute-done.5
  70.7 18.1 %fusion.2 = (f32[8,8,4,64,128]{4,3,2,1,0:T(8,128)}, f32[8,8,4,64,128]{4,3,2,1,0:T(8,128)}) fusion(bf16[3,3,3,32,64]{4,3,2,1,0:T(8,128)(2,1)S(1)} %copy-done.8, bf16[10,10,1,32,128]{4,3,2,1,0:T(8,128)(2,1)S(1)} %collective-permute-done.5, bf16[10,1,4,32,128]{4,3,2,1,0:T(8,128)(2,1)S(1)} %collective-permute-done.3, ...), kind=kOutput, calls=%fused_computation.4 | convolution fusion | flops 3652583424 | bytes 21803008 | tf_op jit(solution)/shard_map/conv_general_dilated | solution.py:42
  88.8 4.4 reduce_sum.18
  93.9 13.5 %all_to_all.24 = bf16[1,4,4,2,64,128]{5,3,2,1,0,4:T(2,128)(2,1)S(1)} all-to-all(bf16[1,4,4,2,64,128]{5,3,2,1,0,4:T(2,128)(2,1)S(1)} %copy.45), channel_id=1, replica_groups=mesh['gx'=4,'gy'=4,'gz'=8] {'gy','gz'}, dimensions={4} | all-to-all | bytes 1048576 | tf_op jit(solution)/shard_map/all_to_all | solution.py:107
  107.6 13.7 %fusion.7 = f32[2048,128]{0,1:T(8,128)} fusion(bf16[4,4,4,8,2,2,2048]{6,5,4,3,2,1,0:T(2,128)(2,1)} %bitcast.74, bf16[32,1,4,4,2,2,128]{6,5,0,4,3,2,1:T(2,128)(2,1)S(1)} %bitcast.72), kind=kOutput, calls=%fused_computation.14 | convolution fusion | flops 1073741824 | bytes 9961472 | tf_op jit(solution)/shard_map/uvxyzcb,xuyvzch->hb/dot_general | solution.py:112
  121.8 145.4 %all-reduce.2.cloned.1.call-done = f32[2048,128]{0,1:T(8,128)} async-done(((f32[2048,128]{0,1:T(8,128)}), f32[2048,128]{0,1:T(8,128)}) %all-reduce.2.cloned.1.call-update) | async-done | bytes 1048592 | tf_op jit(solution)/shard_map/psum | solution.py:115
  270.9 3.5 fusion.12
  274.5 8.6 %fusion.16 = bf16[4,8,4,4,2,2,128]{6,1,5,4,3,0,2:T(8,128)(2,1)S(1)} fusion(bf16[2048,128,1,1,1,1,1]{0,1,6,5,4,3,2:T(8,128)(2,1)S(1)} %fusion.12, bf16[4,4,4,8,2,2,2048]{6,5,4,3,2,1,0:T(2,128)(2,1)} %bitcast.75), kind=kOutput, calls=%fused_computation.21 | convolution fusion | flops 1074003968 | bytes 9437184 | tf_op jit(solution)/shard_map/xuyvzch,hb->uvxyzcb/dot_general | solution.py:132
  283.8 17.7 %all_to_all.25 = bf16[32,4,4,2,2,128]{5,4,3,2,1,0:T(2,128)(2,1)S(1)} all-to-all(bf16[32,4,4,2,2,128]{5,4,3,2,1,0:T(2,128)(2,1)S(1)} %copy.56), channel_id=1, replica_groups=mesh['gx'=4,'gy'=4,'gz'=8] {'gy','gz'}, dimensions={0} | all-to-all | bytes 1048576 | tf_op jit(solution)/shard_map/all_to_all | solution.py:136
  309.7 15.5 %fusion.61 = f32[3,3,3,32,64]{4,3,2,1,0:T(8,128)} fusion(bf16[8,8,4,64,128]{4,3,2,1,0:T(8,128)(2,1)S(1)} %multiply_convert_fusion.1, bf16[10,10,1,32,128]{4,3,2,1,0:T(8,128)(2,1)S(1)} %copy-done.13, bf16[10,1,4,32,128]{4,3,2,1,0:T(8,128)(2,1)S(1)} %copy-done.7, bf16[10,8,4,32,128]{4,3,2,1,0:T(8,128)(2,1)S(1)} %copy-done.5, ...), kind=kOutput, calls=%fused_computation.83 | convolution fusion | flops 3633709056 | bytes 9330688 | tf_op jit(solution)/shard_map/conv_general_dilated | solution.py:65
  325.2 31.7 %fusion.70 = (bf16[10,10,6,32,128]{4,3,2,1,0:T(8,128)(2,1)S(1)}, f32[10,10,6,32,128]{4,3,2,1,0:T(8,128)S(1)}) fusion(bf16[8,8,4,64,128]{4,3,2,1,0:T(8,128)(2,1)} %copy-done.2, bf16[3,3,3,32,64]{4,3,2,1,0:T(8,128)(2,1)S(1)} %copy-done.9), kind=kOutput, calls=%fused_computation.92 | convolution fusion | flops 3626336256 | bytes 19050496 | tf_op jit(solution)/shard_map/conv_general_dilated | solution.py:54
  361.6 7.7 %collective-permute-done.6 = bf16[1,10,6,32,128]{4,3,2,1,0:T(8,128)(2,1)S(1)} collective-permute-done((bf16[1,10,6,32,128]{4,3,2,1,0:T(8,128)(2,1)S(1)}, bf16[1,10,6,32,128]{4,3,2,1,0:T(8,128)(2,1)S(1)}, u32[]{:S(2)}, u32[]{:S(2)}) %collective-permute-start.6) | collective-permute-done | bytes 491552 | tf_op jit(solution)/shard_map/ppermute | solution.py:26
  369.2 4.0 collective-permute-done.7
  374.2 3.7 collective-permute-start.8
  381.9 4.5 collective-permute-done.8
  386.4 11.9 %collective-permute-done.9 = bf16[8,1,6,32,128]{4,3,2,1,0:T(8,128)(2,1)S(1)} collective-permute-done((bf16[8,1,6,32,128]{4,3,2,1,0:T(8,128)(2,1)S(1)}, bf16[8,1,6,32,128]{4,3,2,1,0:T(8,128)(2,1)S(1)}, u32[]{:S(2)}, u32[]{:S(2)}) %collective-permute-start.9) | collective-permute-done | bytes 393248 | tf_op jit(solution)/shard_map/ppermute | solution.py:26
  404.1 9.4 %copy.52 = bf16[4,4,4,8,2,2,2048]{6,5,4,3,2,1,0:T(2,128)(2,1)} copy(bf16[4,4,4,8,2,2,2048]{6,3,5,4,2,0,1:T(8,128)(2,1)S(1)} %fusion) | data formatting | bytes 16777216 | tf_op jit(solution)/shard_map/convert_element_type | solution.py:131
  417.5 291.8 %all-gather.3.cloned.1.call-done = f32[384,3,3,32,64]{4,3,2,1,0:T(8,128)} async-done(((f32[3,3,3,32,64]{4,3,2,1,0:T(8,128)}), f32[384,3,3,32,64]{4,3,2,1,0:T(8,128)}) %all-gather.3.cloned.1.call-update) | async-done | bytes 28311568 | tf_op jit(solution)/shard_map/all_gather | solution.py:154
  709.3 18.2 %reduce_sum.19 = f32[3,3,3,32,64]{4,3,2,1,0:T(8,128)S(1)} reduce(f32[128,3,3,3,32,64]{5,4,3,2,1,0:T(8,128)} %bitcast.64, f32[]{:T(128)} %constant.9.clone.1), dimensions={0}, to_apply=%region_2.3 | reduce | flops 7022592 | bytes 28532740 | tf_op jit(solution)/shard_map/reduce_sum | solution.py:154
  (95 shorter events, 47.2 us)
Async XLA Ops:
  7.2 260.1 %copy-start = (f32[2048,256]{1,0:T(8,128)S(1)}, f32[2048,256]{1,0:T(8,128)}, u32[]{:S(2)}) copy-start(f32[2048,256]{1,0:T(8,128)} %param.9) | copy-start | bytes 6291460
  7.2 260.1 %all-reduce.2.cloned.1.call-start = ((), (), s32[]{:S(2)}) async-start(), calls=%async_computation.2 | async-start | bytes 2097152 | tf_op jit(solution)/shard_map/psum | solution.py:115
  8.4 9.0 %collective-permute-start = (bf16[1,8,4,32,128]{4,3,2,1,0:T(8,128)(2,1)S(1)}, bf16[1,8,4,32,128]{4,3,2,1,0:T(8,128)(2,1)S(1)}, u32[]{:S(2)}, u32[]{:S(2)}) collective-permute-start(bf16[1,8,4,32,128]{4,3,2,1,0:T(8,128)(2,1)S(1)} %get-tuple-element.21), channel_id=1, source_target_pairs={{0,32},{32,64},{64,96},{1,33},{33,65},{65,97},{2,34},{34,66},{66,9... | collective-permute-start | bytes 786440 | tf_op jit(solution)/shard_map/ppermute | solution.py:17
  12.5 8.8 %collective-permute-start.1 = (bf16[1,8,4,32,128]{4,3,2,1,0:T(8,128)(2,1)S(1)}, bf16[1,8,4,32,128]{4,3,2,1,0:T(8,128)(2,1)S(1)}, u32[]{:S(2)}, u32[]{:S(2)}) collective-permute-start(bf16[1,8,4,32,128]{4,3,2,1,0:T(8,128)(2,1)S(1)} %get-tuple-element.20), channel_id=1, source_target_pairs={{32,0},{64,32},{96,64},{33,1},{65,33},{97,65},{34,2},{66,34},{98,6... | collective-permute-start | bytes 786440 | tf_op jit(solution)/shard_map/ppermute | solution.py:18
  17.5 53.2 %copy-start.8 = (bf16[3,3,3,32,64]{4,3,2,1,0:T(8,128)(2,1)S(1)}, bf16[3,3,3,32,64]{4,3,2,1,0:T(8,128)(2,1)}, u32[]{:S(2)}) copy-start(bf16[3,3,3,32,64]{4,3,2,1,0:T(8,128)(2,1)} %param.7) | copy-start | bytes 331780
  21.3 67.4 %copy-start.4 = (bf16[10,8,4,32,128]{4,3,2,1,0:T(8,128)(2,1)}, bf16[10,8,4,32,128]{4,3,2,1,0:T(8,128)(2,1)S(1)}, u32[]{:S(2)}) copy-start(bf16[10,8,4,32,128]{4,3,2,1,0:T(8,128)(2,1)S(1)} %constant_dynamic-update-slice_fusion) | copy-start | bytes 7864324
  21.4 11.2 %collective-permute-start.2 = (bf16[10,1,4,32,128]{4,3,2,1,0:T(8,128)(2,1)S(1)}, bf16[10,1,4,32,128]{4,3,2,1,0:T(8,128)(2,1)S(1)}, u32[]{:S(2)}, u32[]{:S(2)}) collective-permute-start(bf16[10,1,4,32,128]{4,3,2,1,0:T(8,128)(2,1)S(1)} %get-tuple-element.18), channel_id=1, source_target_pairs={{0,8},{8,16},{16,24},{1,9},{9,17},{17,25},{2,10},{10,18},{18,26},{... | collective-permute-start | bytes 983048 | tf_op jit(solution)/shard_map/ppermute | solution.py:17
  28.6 27.5 %collective-permute-start.3 = (bf16[10,1,4,32,128]{4,3,2,1,0:T(8,128)(2,1)S(1)}, bf16[10,1,4,32,128]{4,3,2,1,0:T(8,128)(2,1)S(1)}, u32[]{:S(2)}, u32[]{:S(2)}) collective-permute-start(bf16[10,1,4,32,128]{4,3,2,1,0:T(8,128)(2,1)S(1)} %get-tuple-element.19), channel_id=1, source_target_pairs={{8,0},{16,8},{24,16},{9,1},{17,9},{25,17},{10,2},{18,10},{26,18},{... | collective-permute-start | bytes 983048 | tf_op jit(solution)/shard_map/ppermute | solution.py:18
  56.1 32.7 %copy-start.6 = (bf16[10,1,4,32,128]{4,3,2,1,0:T(8,128)(2,1)}, bf16[10,1,4,32,128]{4,3,2,1,0:T(8,128)(2,1)S(1)}, u32[]{:S(2)}) copy-start(bf16[10,1,4,32,128]{4,3,2,1,0:T(8,128)(2,1)S(1)} %collective-permute-done.3) | copy-start | bytes 983044
  56.3 10.6 %collective-permute-start.4 = (bf16[10,10,1,32,128]{4,3,2,1,0:T(8,128)(2,1)S(1)}, bf16[10,10,1,32,128]{4,3,2,1,0:T(8,128)(2,1)S(1)}, u32[]{:S(2)}, u32[]{:S(2)}) collective-permute-start(bf16[10,10,1,32,128]{4,3,2,1,0:T(8,128)(2,1)S(1)} %get-tuple-element.14), channel_id=1, source_target_pairs={{0,1},{1,2},{2,3},{3,4},{4,5},{5,6},{6,7},{8,9},{9,10},{10,11},{11... | collective-permute-start | bytes 2457608 | tf_op jit(solution)/shard_map/ppermute | solution.py:17
  57.6 13.1 %collective-permute-start.5 = (bf16[10,10,1,32,128]{4,3,2,1,0:T(8,128)(2,1)S(1)}, bf16[10,10,1,32,128]{4,3,2,1,0:T(8,128)(2,1)S(1)}, u32[]{:S(2)}, u32[]{:S(2)}) collective-permute-start(bf16[10,10,1,32,128]{4,3,2,1,0:T(8,128)(2,1)S(1)} %get-tuple-element.15), channel_id=1, source_target_pairs={{1,0},{2,1},{3,2},{4,3},{5,4},{6,5},{7,6},{9,8},{10,9},{11,10},{12... | collective-permute-start | bytes 2457608 | tf_op jit(solution)/shard_map/ppermute | solution.py:18
  66.8 21.9 %copy-start.10 = (bf16[10,10,1,32,128]{4,3,2,1,0:T(8,128)(2,1)}, bf16[10,10,1,32,128]{4,3,2,1,0:T(8,128)(2,1)S(1)}, u32[]{:S(2)}) copy-start(bf16[10,10,1,32,128]{4,3,2,1,0:T(8,128)(2,1)S(1)} %collective-permute-done.4) | copy-start | bytes 2457604
  70.7 18.1 %copy-start.12 = (bf16[10,10,1,32,128]{4,3,2,1,0:T(8,128)(2,1)}, bf16[10,10,1,32,128]{4,3,2,1,0:T(8,128)(2,1)S(1)}, u32[]{:S(2)}) copy-start(bf16[10,10,1,32,128]{4,3,2,1,0:T(8,128)(2,1)S(1)} %collective-permute-done.5) | copy-start | bytes 2457604
  107.6 162.7 %copy-start.14 = (f32[256,4]{0,1:T(4,128)S(1)}, f32[256,4]{0,1:T(4,128)}, u32[]{:S(2)}) copy-start(f32[256,4]{0,1:T(4,128)} %param.10) | copy-start | bytes 12292
  107.6 162.9 %copy-start.15 = (f32[4,128]{1,0:T(4,128)S(1)}, f32[4,128]{1,0:T(4,128)}, u32[]{:S(2)}) copy-start(f32[4,128]{1,0:T(4,128)} %param.11) | copy-start | bytes 6148
  121.4 588.0 %all-gather.3.cloned.1.call-start = ((), (), s32[]{:S(2)}) async-start(), calls=%async_computation.3 | async-start | bytes 57065472 | tf_op jit(solution)/shard_map/all_gather | solution.py:154
  283.2 20.5 %slice-start.1 = ((s8[8388608]{0:T(1024)(128)(4,1)}), s8[4194304]{0:T(1024)(128)(4,1)S(1)}, s32[]{:S(2)}) async-start(s8[8388608]{0:T(1024)(128)(4,1)} %bitcast.67), calls=%async_computation.5 | async-start | bytes 8388608
  357.0 12.2 %collective-permute-start.6 = (bf16[1,10,6,32,128]{4,3,2,1,0:T(8,128)(2,1)S(1)}, bf16[1,10,6,32,128]{4,3,2,1,0:T(8,128)(2,1)S(1)}, u32[]{:S(2)}, u32[]{:S(2)}) collective-permute-start(bf16[1,10,6,32,128]{4,3,2,1,0:T(8,128)(2,1)S(1)} %get-tuple-element.10), channel_id=1, source_target_pairs={{0,32},{32,64},{64,96},{1,33},{33,65},{65,97},{2,34},{34,66},{66,9... | collective-permute-start | bytes 1474568 | tf_op jit(solution)/shard_map/ppermute | solution.py:26
  359.1 14.1 %collective-permute-start.7 = (bf16[1,10,6,32,128]{4,3,2,1,0:T(8,128)(2,1)S(1)}, bf16[1,10,6,32,128]{4,3,2,1,0:T(8,128)(2,1)S(1)}, u32[]{:S(2)}, u32[]{:S(2)}) collective-permute-start(bf16[1,10,6,32,128]{4,3,2,1,0:T(8,128)(2,1)S(1)} %get-tuple-element.11), channel_id=1, source_target_pairs={{32,0},{64,32},{96,64},{33,1},{65,33},{97,65},{34,2},{66,34},{98,6... | collective-permute-start | bytes 1474568 | tf_op jit(solution)/shard_map/ppermute | solution.py:26
  374.2 12.2 %collective-permute-start.8 = (bf16[8,1,6,32,128]{4,3,2,1,0:T(8,128)(2,1)S(1)}, bf16[8,1,6,32,128]{4,3,2,1,0:T(8,128)(2,1)S(1)}, u32[]{:S(2)}, u32[]{:S(2)}) collective-permute-start(bf16[8,1,6,32,128]{4,3,2,1,0:T(8,128)(2,1)S(1)} %get-tuple-element.12), channel_id=1, source_target_pairs={{0,8},{8,16},{16,24},{1,9},{9,17},{17,25},{2,10},{10,18},{18,26},{... | collective-permute-start | bytes 1179656 | tf_op jit(solution)/shard_map/ppermute | solution.py:26
  377.9 20.4 %collective-permute-start.9 = (bf16[8,1,6,32,128]{4,3,2,1,0:T(8,128)(2,1)S(1)}, bf16[8,1,6,32,128]{4,3,2,1,0:T(8,128)(2,1)S(1)}, u32[]{:S(2)}, u32[]{:S(2)}) collective-permute-start(bf16[8,1,6,32,128]{4,3,2,1,0:T(8,128)(2,1)S(1)} %get-tuple-element.13), channel_id=1, source_target_pairs={{8,0},{16,8},{24,16},{9,1},{17,9},{25,17},{10,2},{18,10},{26,18},{... | collective-permute-start | bytes 1179656 | tf_op jit(solution)/shard_map/ppermute | solution.py:26
  399.1 15.6 %collective-permute-start.10 = (bf16[8,8,1,32,128]{4,3,2,1,0:T(8,128)(2,1)S(1)}, bf16[8,8,1,32,128]{4,3,2,1,0:T(8,128)(2,1)S(1)}, u32[]{:S(2)}, u32[]{:S(2)}) collective-permute-start(bf16[8,8,1,32,128]{4,3,2,1,0:T(8,128)(2,1)S(1)} %get-tuple-element.16), channel_id=1, source_target_pairs={{0,1},{1,2},{2,3},{3,4},{4,5},{5,6},{6,7},{8,9},{9,10},{10,11},{11... | collective-permute-start | bytes 1572872 | tf_op jit(solution)/shard_map/ppermute | solution.py:26
  400.5 14.3 %collective-permute-start.11 = (bf16[8,8,1,32,128]{4,3,2,1,0:T(8,128)(2,1)S(1)}, bf16[8,8,1,32,128]{4,3,2,1,0:T(8,128)(2,1)S(1)}, u32[]{:S(2)}, u32[]{:S(2)}) collective-permute-start(bf16[8,8,1,32,128]{4,3,2,1,0:T(8,128)(2,1)S(1)} %get-tuple-element.17), channel_id=1, source_target_pairs={{1,0},{2,1},{3,2},{4,3},{5,4},{6,5},{7,6},{9,8},{10,9},{11,10},{12... | collective-permute-start | bytes 1572872 | tf_op jit(solution)/shard_map/ppermute | solution.py:26
  709.3 19.0 %copy-start.1 = (f32[2048,256]{1,0:T(8,128)S(1)}, f32[2048,256]{1,0:T(8,128)}, u32[]{:S(2)}) copy-start(f32[2048,256]{1,0:T(8,128)} %param.9) | copy-start | bytes 6291460
  (12 other events, 79.3 us)
Sparse Core Ops, SparseCore 0:
  121.5 145.7 all-reduce.1
  325.4 383.9 all-gather.2
